TPU v7x, 32 devices: a whole 2x2x4 slice. The times are simulated.
32 devices in a mesh: expert: 8 (over y, x, core), row: 4 (over z).
Axes of the slice: x: 2, y: 2, z: 4, core: 2. Of those that a mesh axis runs over, the one named last changes fastest.
Arguments:
- weights: bfloat16 [8, 7168, 2048], P('expert', 'row'), may hold values from -6 to 6
- left_bits: int32 [8, 7168], P('expert', 'row'), may hold values from 0 to 1
- right_bits: int32 [8, 2048], P('expert'), may hold values from 0 to 1
- groups: int32 [8, 2048], P('expert'), may hold values from 0 to 15, never falling along the last dimension, each value on 1 to 256 neighbouring positions
Outputs:
- scaled: bfloat16 [8, 7168, 2048], P('expert', 'row')
- block_error: float32 [8, 7168, 256], P('expert', 'row')
- scales: float32 [8, 16], P('expert')
- expert_error: float32 [8], P('expert')
- total_error: float32 [], replicated
Inputs may be any that keep to these rules, and one draw needn't show every extreme that they name: Along each expert's 2048 columns the group number never falls; each of the 16 groups holds 1 to 256 columns.
All inputs are finite; a program needn't handle non-finite values.
Results may differ from a plain program's by a relative error of at most 0.0091.
Values may be sent and summed in bfloat16 or wider, within the bound.
No kernel may reach another device: no remote copies, remote signals or barrier semaphores. Data moves between devices by JAX's collectives and lax.ppermute only.
A program may use at most 192 MiB of HBM per device.

v0:
```python
import math
import jax
import jax.numpy as jnp
from jax import lax
from jax.sharding import PartitionSpec as P

D = 7168
FF = 2048
HB = 128
OUTER = 16
GROUPS = 16
BLOCKS = 56


def sylvester(order):
    row_index = jnp.arange(order, dtype=jnp.int32)[:, None]
    col_index = jnp.arange(order, dtype=jnp.int32)[None, :]
    common = jnp.bitwise_and(row_index, col_index)
    parity = jnp.zeros((order, order), jnp.int32)
    for bit_pos in range(order.bit_length() - 1):
        parity = parity + jnp.bitwise_and(jnp.right_shift(common, bit_pos), 1)
    return (1 - 2 * jnp.bitwise_and(parity, 1)).astype(jnp.float32)


def cosine_block(order):
    first = jnp.arange(order, dtype=jnp.float32)[:, None]
    second = jnp.arange(order, dtype=jnp.float32)[None, :]
    table = math.sqrt(2.0 / order) * jnp.cos(math.pi * (2.0 * second + 1.0) * first / (2.0 * order))
    return jnp.where(first == 0.0, table * math.sqrt(0.5), table)


def coset_error(values):
    nearest = jnp.floor(values + 0.5)
    offset = values - nearest
    squares = jnp.sum(offset * offset, axis=-1)
    largest = jnp.max(jnp.abs(offset), axis=-1)
    parity = jnp.mod(jnp.sum(nearest, axis=-1), 2.0)
    return jnp.where(parity > 0.5, squares + 1.0 - 2.0 * largest, squares)


def lattice_error(values):
    octets = values.reshape(values.shape[:-1] + (values.shape[-1] // 8, 8))
    return jnp.minimum(coset_error(octets), coset_error(octets - 0.5))


def row_transform(mixed_rows, row_hadamard):
    turned = jnp.einsum("eibf,bk->eikf", mixed_rows, row_hadamard, precision=lax.Precision.HIGHEST)
    return turned / math.sqrt(HB)


def weight_of_rows(first_row, count):
    positions = (first_row + jnp.arange(count, dtype=jnp.int32)).astype(jnp.float32)
    return (1.0 + 4.0 * (positions + 0.5) / D) / 3.0


def group_scale(rotated, group_cols):
    column_peak = jnp.max(jnp.abs(rotated), axis=1)
    group_ids = jnp.arange(GROUPS, dtype=jnp.int32)
    in_group = group_cols[:, None, :] == group_ids[None, :, None]
    partial_peak = jnp.max(jnp.where(in_group, column_peak[:, None, :], 0.0), axis=2)
    group_peak = jnp.maximum(lax.pmax(partial_peak, "row"), 1.0)
    column_scale = jnp.sum(jnp.where(in_group, (2.0 / group_peak)[:, :, None], 0.0), axis=1)
    return (group_peak, column_scale)


def body(weights, left_bits, right_bits, groups):
    experts, local_rows, width = weights.shape
    blocks_here = local_rows // HB
    column_hadamard = sylvester(width // OUTER).astype(jnp.bfloat16)
    outer_hadamard = sylvester(OUTER)
    row_hadamard = sylvester(HB)
    block_matrix = cosine_block(BLOCKS).astype(jnp.bfloat16)
    left_sign = (2 * left_bits - 1).astype(jnp.float32)
    right_sign = (2 * right_bits - 1).astype(jnp.float32)
    signed = (weights.astype(jnp.float32) * left_sign[:, :, None] * right_sign[:, None, :]).astype(
        jnp.bfloat16
    )
    shaped = signed.reshape(experts, local_rows, OUTER, width // OUTER)
    inner = jnp.einsum("erpq,qs->erps", shaped, column_hadamard, preferred_element_type=jnp.float32)
    outer = jnp.einsum("erps,pt->erts", inner, outer_hadamard, precision=lax.Precision.HIGHEST)
    columns = (outer.reshape(experts, local_rows, width) / math.sqrt(FF)).astype(jnp.bfloat16)
    blocked = columns.reshape(experts, blocks_here, HB, width)
    own_start = lax.axis_index("row") * blocks_here
    own_matrix = lax.dynamic_slice_in_dim(block_matrix, own_start, blocks_here, 0)
    mixed_rows = jnp.einsum(
        "ij,ejbf->eibf",
        own_matrix,
        lax.all_gather(blocked, "row", axis=1, tiled=True),
        preferred_element_type=jnp.float32,
    )
    rotated = row_transform(mixed_rows, row_hadamard)
    rotated = rotated.reshape(experts, local_rows, width)
    group_peak, column_scale = group_scale(rotated, groups)
    values = rotated * column_scale[:, None, :]
    block_errors = lattice_error(values)
    row_weight = weight_of_rows(lax.axis_index("row") * local_rows, local_rows)
    partial_error = jnp.sum(block_errors * row_weight[None, :, None], axis=(1, 2)) / (D * FF // 8)
    scaled = values.astype(jnp.bfloat16)
    expert_count = experts * lax.axis_size("expert")
    expert_error = lax.psum(partial_error, "row")
    total_error = lax.psum(jnp.sum(expert_error), "expert") / expert_count
    return (scaled, block_errors, group_peak / 2.0, expert_error, total_error)


def solution(mesh):
    placed = (P("expert", "row", None), P("expert", "row"), P("expert", None), P("expert", None))
    return jax.shard_map(
        body,
        mesh=mesh,
        in_specs=placed,
        out_specs=(
            P("expert", "row", None),
            P("expert", "row", None),
            P("expert", None),
            P("expert"),
            P(),
        ),
        check_vma=False,
    )
```

profile of v0, /device:TPU:0, one launch (start us, length us, event | category | flops | bytes accessed | tf_op | source)
XLA Modules:
  0.0 734.2 jit_solution(6547402217888224501)
XLA Ops:
  7.2 0.0 all-gather.2.cloned.1.call-start
  7.2 0.7 add_convert_fusion
  7.9 0.7 convert_reduce_fusion
  8.6 5.1 fusion.8
  13.7 5.8 copy.28
  19.5 4.3 fusion.25
  23.9 15.7 %fusion.14 = bf16[1,1792,16,128]{3,2,1,0:T(8,128)(2,1)} fusion(f32[1792,16,128]{2,1,0:T(8,128)S(1)} %fusion.25), kind=kOutput, calls=%fused_computation.22 | convolution fusion | flops 711987200 | bytes 22020096 | tf_op jit(solution)/shard_map/erps,pt->erts/dot_general | solution.py:80
  39.6 11.8 %convert_element_type.76 = bf16[1,14,128,2048]{3,2,1,0:T(8,128)(2,1)} reshape(bf16[1,1792,16,128]{3,2,1,0:T(8,128)(2,1)} %fusion.14) | data formatting | bytes 14680064 | tf_op jit(solution)/shard_map/convert_element_type | solution.py:81
  51.4 0.0 all-gather.2.cloned.1.call-update
  51.4 0.1 dynamic-slice
  51.5 495.9 %all-gather.2.cloned.1.call-done = bf16[1,56,128,2048]{3,2,0,1:T(8,128)(2,1)} async-done(((bf16[1,14,128,2048]{3,2,0,1:T(8,128)(2,1)}), bf16[1,56,128,2048]{3,2,0,1:T(8,128)(2,1)}) %all-gather.2.cloned.1.call-update) | async-done | bytes 29360144 | tf_op jit(solution)/shard_map/all_gather | solution.py:88
  547.4 31.9 %fusion.9 = f32[14,128,2048]{2,0,1:T(8,128)} fusion(bf16[1,56,128,2048]{3,2,0,1:T(8,128)(2,1)} %all-gather.2.cloned.1.call-done, s32[]{:T(128)S(6)} %select_n.94, f32[56]{0:T(128)S(1)} %add_multiply_fusion.2, pred[14]{0:T(512)(128)(4,1)S(1)} %dynamic-slice), kind=kOutput, calls=%fused_computation.21 | convolution fusion | flops 411048064 | bytes 44040432 | tf_op jit(solution)/shard_map/ij,ejbf->eibf/dot_general | solution.py:85
  579.3 0.0 copy-start
  579.3 29.6 %abs_reduce_fusion.2 = (f32[2048]{0:T(1024)S(1)}, f32[128,14,2048]{2,0,1:T(8,128)}) fusion(f32[14,128,2048]{2,0,1:T(8,128)} %fusion.9), kind=kOutput, calls=%fused_computation.15 | convolution fusion | flops 5648562176 | bytes 29368320 | tf_op jit(solution)/shard_map/eibf,bk->eikf/dot_general | solution.py:47
  608.9 0.0 copy-done
  608.9 0.1 select_reduce_fusion.1
  609.0 8.9 %pmax.7 = f32[1,16]{1,0:T(1,128)S(1)} all-reduce(f32[1,16]{1,0:T(1,128)S(1)} %bitcast.114), channel_id=1, replica_groups=mesh['expert'=8,'row'=4] {'row'}, use_global_device_ids=true, to_apply=%region_2.3 | all-reduce | flops 16 | bytes 128 | tf_op jit(solution)/shard_map/pmax | solution.py:61
  617.9 0.5 maximum_multiply_fusion
  618.4 0.1 select_reduce_fusion
  618.5 0.1 mul.276
  618.6 10.4 %fusion.3 = bf16[1,1792,2048]{2,1,0:T(8,128)(2,1)} fusion(f32[128,14,2048]{2,0,1:T(8,128)} %get-tuple-element.26, f32[2048]{0:T(1024)S(1)} %select_reduce_fusion), kind=kLoop, calls=%fused_computation.4 | loop fusion | flops 7340032 | bytes 22028288 | tf_op jit(solution)/shard_map/convert_element_type | solution.py:98
  629.0 17.6 %copy.24 = f32[1,14,128,2048]{2,1,3,0:T(8,128)} copy(f32[1,14,128,2048]{3,2,1,0:T(8,128)} %bitcast.108) | data formatting | bytes 29360128 | tf_op jit(solution)/shard_map/div | solution.py:48
  646.6 16.9 %reshape.599 = f32[1,1792,256,8]{1,3,2,0:T(8,128)} reshape(f32[1,14,128,2048]{2,1,3,0:T(8,128)} %copy.24) | data formatting | bytes 29360128 | tf_op jit(solution)/shard_map/reshape | solution.py:92
  663.5 32.5 %fusion.7 = (f32[1792,256]{0,1:T(8,128)S(1)}, f32[1792,256]{0,1:T(8,128)S(1)}, f32[1792,256]{0,1:T(8,128)S(1)}, f32[1792,256]{0,1:T(8,128)S(1)}, f32[1792,256]{0,1:T(8,128)S(1)}, /*index=5*/f32[1792,256]{0,1:T(8,128)S(1)}) fusion(f32[1,1792,256,8]{1,3,2,0:T(8,128)} %reshape.599, f32[256,8]{1,0:T(8,128)S(1)} %mul.276), kind=kLoop, calls=%fused_computation.14 | loop fusion | flops 59637760 | bytes 25698304 | tf_op jit(solution)/shard_map/reduce_sum | solution.py:37
  696.0 3.2 multiply_reduce_fusion.2
  699.3 1.7 copy.25
  701.6 11.3 %psum.14 = f32[1]{0:T(128)} all-reduce(f32[1]{0:T(128)} %bitcast.25), channel_id=1, replica_groups=mesh['expert'=8,'row'=4] {'row'}, use_global_device_ids=true, to_apply=%region_11.12 | all-reduce | flops 1 | bytes 8 | tf_op jit(solution)/shard_map/psum | solution.py:100
  712.9 12.4 %psum.15 = f32[]{:T(128)} all-reduce(f32[]{:T(128)} %bitcast.26), channel_id=1, replica_groups=mesh['expert'=8,'row'=4] {'expert'}, use_global_device_ids=true, to_apply=%region_12.13 | all-reduce | flops 1 | bytes 8 | tf_op jit(solution)/shard_map/psum | solution.py:101
  (3 shorter events, 0.0 us)
Async XLA Ops:
  7.2 540.2 %all-gather.2.cloned.1.call-start = ((), (), s32[]{:S(2)}) async-start(), calls=%async_computation | async-start | bytes 36700160 | tf_op jit(solution)/shard_map/all_gather | solution.py:88
  579.3 29.6 %copy-start = (s32[1,2048]{1,0:T(1,128)S(1)}, s32[1,2048]{1,0:T(1,128)}, u32[]{:S(2)}) copy-start(s32[1,2048]{1,0:T(1,128)} %param.7) | copy-start | bytes 24580
Sparse Core Ops, SparseCore 0:
  51.5 495.8 all-gather.1
where the time goes:
time: 743 us; the launch traced here: 734 us
  waiting for transfers between devices  496 us (67%)
  matrix products  81.6 us (11%)
  local copies, waits for them, and re-layouts  53.9 us (7%)
  other arithmetic  53.5 us (7%)
  blocking collectives  32.6 us (4%)
  between operations  16.7 us (2%)
    all_gather x1, waiting for transfers between devices, body(): lax.all_gather(blocked, 'row', axis=1, tiled=True)  496 us
    reduce_sum x1, other arithmetic, coset_error(): parity = jnp.mod(jnp.sum(nearest, axis=-1), 2.0)  32.5 us
    dot_general x1, matrix products, body(): jnp.einsum('ij,ejbf->eibf', own_matrix, lax.all_gather(blocked, 'row', ax...  31.9 us
    dot_general x1, matrix products, row_transform(): jnp.einsum('eibf,bk->eikf', mixed_rows, row_hadamard, precision=lax.Preci...  29.6 us
    div x1, local copies, waits for them, and re-layouts, row_transform(): return turned / math.sqrt(HB)  17.6 us
    reshape x1, local copies, waits for them, and re-layouts, body(): rotated = rotated.reshape(experts, local_rows, width)  16.9 us
    dot_general x1, matrix products, body(): jnp.einsum('erps,pt->erts', inner, outer_hadamard, precision=lax.Precisio...  15.7 us
  transfers between devices with their start and end apart: 1, of which 1 were waited for; matrix products, arithmetic and copies ran while one was open for 0% of the time, Pallas kernels for 0%

commit v1 on v0

--- a/solution.py
+++ b/solution.py
@@ -82,11 +82,32 @@
     blocked = columns.reshape(experts, blocks_here, HB, width)
     own_start = lax.axis_index("row") * blocks_here
     own_matrix = lax.dynamic_slice_in_dim(block_matrix, own_start, blocks_here, 0)
-    mixed_rows = jnp.einsum(
-        "ij,ejbf->eibf",
-        own_matrix,
-        lax.all_gather(blocked, "row", axis=1, tiled=True),
-        preferred_element_type=jnp.float32,
+
+    def post_ticks_in(content, m):
+        piece_now, z_new, low = (lax.axis_size("row"), lax.axis_index("row"), content.shape[1])
+        shelf = tuple(((w, (w + 1) % piece_now) for w in range(piece_now)))
+        store = tuple(((w, (w - 1) % piece_now) for w in range(piece_now)))
+        passed = piece_now // 2
+        w2 = raw_out = content
+        mid_arr = m(content, z_new * low)
+        at = 1
+        while at < passed + 1:
+            w2 = lax.ppermute(w2, axis_name="row", perm=shelf)
+            if at < piece_now - passed:
+                raw_out = lax.ppermute(raw_out, perm=store, axis_name="row")
+                mid_arr = mid_arr + m(raw_out, (z_new + at) % piece_now * low)
+            mid_arr = mid_arr + m(w2, (z_new - at) % piece_now * low)
+            at += 1
+        return mid_arr
+
+    mixed_rows = post_ticks_in(
+        blocked,
+        lambda own_block, offset_2: jnp.einsum(
+            "ij,ejbf->eibf",
+            lax.dynamic_slice_in_dim(own_matrix, offset_2, own_block.shape[1], axis=1),
+            own_block,
+            preferred_element_type=jnp.float32,
+        ),
     )
     rotated = row_transform(mixed_rows, row_hadamard)
     rotated = rotated.reshape(experts, local_rows, width)

time: 743 us -> 712 us (0.958)
  waiting for transfers between devices: 496 us -> 421 us
  matrix products: 81.6 us -> 122 us
  between operations: 16.7 us -> 3.38 us
  local copies, waits for them, and re-layouts: 53.9 us -> 65.9 us
    all_gather x1 -> x0, waiting for transfers between devices: 496 us -> none  [body(): lax.all_gather(blocked, 'row', axis=1, tiled=True)]
    ppermute x0 -> x3, waiting for transfers between devices: none -> 421 us  [the longest x2 303 us: post_ticks_in(): w2 = lax.ppermute(w2, axis_name='row', perm=shelf)]
    dot_general x1 -> x4, matrix products: 31.9 us -> 72 us  [body(): jnp.einsum('ij,ejbf->eibf', lax.dynamic_slice_in_dim(own_matrix, offset_2...]
    convert_element_type x1 -> x2, local copies, waits for them, and re-layouts: 11.8 us -> 23.8 us  [body(): (outer.reshape(experts, local_rows, width) / math.sqrt(FF)).astype(jnp.bf...]
  transfers between devices with their start and end apart: 1 -> 3, of which waited for: 1 -> 3; matrix products, arithmetic and copies ran while one was open for 0% -> 7% of each run, Pallas kernels for 0% -> 0%
where the time goes in v1:
time: 712 us; the launch traced here: 703 us
  waiting for transfers between devices  421 us (59%)
  matrix products  122 us (17%)
  local copies, waits for them, and re-layouts  65.9 us (9%)
  other arithmetic  53.6 us (8%)
  blocking collectives  32.5 us (5%)
    ppermute x2, waiting for transfers between devices, post_ticks_in(): w2 = lax.ppermute(w2, axis_name='row', perm=shelf)  303 us
    ppermute x1, waiting for transfers between devices, post_ticks_in(): raw_out = lax.ppermute(raw_out, perm=store, axis_name='row')  117 us
    dot_general x4, matrix products, body(): jnp.einsum('ij,ejbf->eibf', lax.dynamic_slice_in_dim(own_matrix, offset_2...  72 us
    reduce_sum x1, other arithmetic, coset_error(): parity = jnp.mod(jnp.sum(nearest, axis=-1), 2.0)  32.5 us
    dot_general x1, matrix products, row_transform(): jnp.einsum('eibf,bk->eikf', mixed_rows, row_hadamard, precision=lax.Preci...  29.8 us
    convert_element_type x2, local copies, waits for them, and re-layouts, body(): (outer.reshape(experts, local_rows, width) / math.sqrt(FF)).astype(jnp.bf...  23.8 us
    div x1, local copies, waits for them, and re-layouts, row_transform(): return turned / math.sqrt(HB)  17.6 us
    reshape x1, local copies, waits for them, and re-layouts, body(): rotated = rotated.reshape(experts, local_rows, width)  16.9 us
  transfers between devices with their start and end apart: 3, of which 3 were waited for; matrix products, arithmetic and copies ran while one was open for 7% of the time, Pallas kernels for 0%

profile of v1, /device:TPU:0, one launch (start us, length us, event | category | flops | bytes accessed | tf_op | source)
XLA Modules:
  0.0 702.9 jit_solution(1040418867652502322)
XLA Ops:
  0.6 0.7 add_convert_fusion
  1.3 0.7 convert_reduce_fusion
  2.1 5.1 fusion.16
  7.1 5.8 copy.36
  12.9 4.3 fusion.32
  17.3 15.7 %fusion.21 = bf16[1,1792,16,128]{3,2,1,0:T(8,128)(2,1)} fusion(f32[1792,16,128]{2,1,0:T(8,128)S(1)} %fusion.32), kind=kOutput, calls=%fused_computation.30 | convolution fusion | flops 711987200 | bytes 22020096 | tf_op jit(solution)/shard_map/erps,pt->erts/dot_general | solution.py:80
  33.0 11.8 %convert_element_type.90 = bf16[1,14,128,2048]{3,2,1,0:T(8,128)(2,1)} reshape(bf16[1,1792,16,128]{3,2,1,0:T(8,128)(2,1)} %fusion.21) | data formatting | bytes 14680064 | tf_op jit(solution)/shard_map/convert_element_type | solution.py:81
  44.8 3.1 collective-permute-start.1
  47.9 2.0 collective-permute-start
  49.9 159.2 %collective-permute-done.1 = bf16[1,14,128,2048]{3,2,1,0:T(8,128)(2,1)} collective-permute-done((bf16[1,14,128,2048]{3,2,1,0:T(8,128)(2,1)}, bf16[1,14,128,2048]{3,2,1,0:T(8,128)(2,1)}, u32[]{:S(2)}, u32[]{:S(2)}) %collective-permute-start.1) | collective-permute-done | bytes 7340064 | tf_op jit(solution)/shard_map/ppermute | solution.py:95
  209.1 12.0 %convert_element_type.88 = bf16[14,128,2048]{2,1,0:T(8,128)(2,1)} reshape(bf16[1,1792,16,128]{3,2,1,0:T(8,128)(2,1)} %fusion.21) | data formatting | bytes 14680064 | tf_op jit(solution)/shard_map/convert_element_type | solution.py:81
  221.2 0.1 select_convert_fusion
  221.3 13.3 %fusion.14 = f32[128,2048,14]{1,2,0:T(8,128)} fusion(bf16[14,128,2048]{2,1,0:T(8,128)(2,1)} %convert_element_type.88, bf16[56,56]{1,0:T(8,128)(2,1)S(1)} %select_convert_fusion, s32[]{:T(128)S(6)} %select_n.134), kind=kOutput, calls=%fused_computation.26 | convolution fusion | flops 102760448 | bytes 22024196 | tf_op jit(solution)/shard_map/ij,ejbf->eibf/dot_general | solution.py:105
  234.6 13.3 %fusion.7 = f32[128,2048,14]{1,2,0:T(8,128)} fusion(bf16[1,14,128,2048]{3,2,1,0:T(8,128)(2,1)} %collective-permute-done.1, bf16[56,56]{1,0:T(8,128)(2,1)S(1)} %select_convert_fusion, s32[]{:T(128)S(6)} %select_n.134, s32[]{:T(128)S(6)} %select_n.140), kind=kOutput, calls=%fused_computation.19 | convolution fusion | flops 102760448 | bytes 22024200 | tf_op jit(solution)/shard_map/ij,ejbf->eibf/dot_general | solution.py:105
  248.0 117.2 %collective-permute-done = bf16[1,14,128,2048]{3,2,1,0:T(8,128)(2,1)} collective-permute-done((bf16[1,14,128,2048]{3,2,1,0:T(8,128)(2,1)}, bf16[1,14,128,2048]{3,2,1,0:T(8,128)(2,1)}, u32[]{:S(2)}, u32[]{:S(2)}) %collective-permute-start) | collective-permute-done | bytes 7340064 | tf_op jit(solution)/shard_map/ppermute | solution.py:97
  365.2 13.5 %fusion.9 = f32[128,2048,14]{1,2,0:T(8,128)} fusion(bf16[1,14,128,2048]{3,2,1,0:T(8,128)(2,1)} %collective-permute-done, bf16[56,56]{1,0:T(8,128)(2,1)S(1)} %select_convert_fusion, s32[]{:T(128)S(6)} %select_n.134, s32[]{:T(128)S(6)} %select_n.137), kind=kOutput, calls=%fused_computation.21 | convolution fusion | flops 102760448 | bytes 22024200 | tf_op jit(solution)/shard_map/ij,ejbf->eibf/dot_general | solution.py:105
  378.7 144.1 %collective-permute-done.2 = bf16[1,14,128,2048]{3,2,1,0:T(8,128)(2,1)} collective-permute-done((bf16[1,14,128,2048]{3,2,1,0:T(8,128)(2,1)}, bf16[1,14,128,2048]{3,2,1,0:T(8,128)(2,1)}, u32[]{:S(2)}, u32[]{:S(2)}) %collective-permute-start.2) | collective-permute-done | bytes 7340064 | tf_op jit(solution)/shard_map/ppermute | solution.py:95
  522.8 31.9 %add_bitcast_fusion = f32[14,128,2048]{2,0,1:T(8,128)} fusion(f32[128,2048,14]{1,2,0:T(8,128)} %fusion.7, f32[128,2048,14]{1,2,0:T(8,128)} %fusion.14, f32[128,2048,14]{1,2,0:T(8,128)} %fusion.9, bf16[1,14,128,2048]{3,2,1,0:T(8,128)(2,1)} %collective-permute-done.2, bf16[56,56]{1,0:T(8,128)(2,1)S(1)} %select_convert_fusion, s32[]{:T(128)S(6)} %select_n.134, ...), kind=kOutput, calls=%fused_computation | convolution fusion | flops 113770496 | bytes 66064392 | tf_op jit(solution)/shard_map/ij,ejbf->eibf/dot_general | solution.py:105
  554.7 29.8 %abs_reduce_fusion.2 = (f32[2048]{0:T(1024)S(1)}, f32[128,14,2048]{2,0,1:T(8,128)}) fusion(f32[14,128,2048]{2,0,1:T(8,128)} %add_bitcast_fusion), kind=kOutput, calls=%fused_computation.13 | convolution fusion | flops 5648562176 | bytes 29368320 | tf_op jit(solution)/shard_map/eibf,bk->eikf/dot_general | solution.py:47
  584.5 0.1 select_reduce_fusion.1
  584.7 10.2 %pmax.7 = f32[1,16]{1,0:T(1,128)S(1)} all-reduce(f32[1,16]{1,0:T(1,128)S(1)} %bitcast.129), channel_id=1, replica_groups=mesh['expert'=8,'row'=4] {'row'}, use_global_device_ids=true, to_apply=%region_2.3 | all-reduce | flops 16 | bytes 128 | tf_op jit(solution)/shard_map/pmax | solution.py:61
  594.9 0.5 maximum_multiply_fusion
  595.4 0.1 select_reduce_fusion
  595.5 0.1 mul.331
  595.6 10.4 %fusion = bf16[1,1792,2048]{2,1,0:T(8,128)(2,1)} fusion(f32[128,14,2048]{2,0,1:T(8,128)} %get-tuple-element.26, f32[2048]{0:T(1024)S(1)} %select_reduce_fusion), kind=kLoop, calls=%fused_computation.2 | loop fusion | flops 7340032 | bytes 22028288 | tf_op jit(solution)/shard_map/convert_element_type | solution.py:119
  606.0 17.6 %copy.32 = f32[1,14,128,2048]{2,1,3,0:T(8,128)} copy(f32[1,14,128,2048]{3,2,1,0:T(8,128)} %bitcast.124) | data formatting | bytes 29360128 | tf_op jit(solution)/shard_map/div | solution.py:48
  623.6 16.9 %reshape.621 = f32[1,1792,256,8]{1,3,2,0:T(8,128)} reshape(f32[1,14,128,2048]{2,1,3,0:T(8,128)} %copy.32) | data formatting | bytes 29360128 | tf_op jit(solution)/shard_map/reshape | solution.py:113
  640.5 32.5 %fusion.4 = (f32[1792,256]{0,1:T(8,128)S(1)}, f32[1792,256]{0,1:T(8,128)S(1)}, f32[1792,256]{0,1:T(8,128)S(1)}, f32[1792,256]{0,1:T(8,128)S(1)}, f32[1792,256]{0,1:T(8,128)S(1)}, /*index=5*/f32[1792,256]{0,1:T(8,128)S(1)}) fusion(f32[1,1792,256,8]{1,3,2,0:T(8,128)} %reshape.621, f32[256,8]{1,0:T(8,128)S(1)} %mul.331), kind=kLoop, calls=%fused_computation.12 | loop fusion | flops 59637760 | bytes 25698304 | tf_op jit(solution)/shard_map/reduce_sum | solution.py:37
  673.0 3.2 multiply_reduce_fusion.2
  676.3 1.7 copy.33
  678.6 9.9 %psum.14 = f32[1]{0:T(128)} all-reduce(f32[1]{0:T(128)} %bitcast.30), channel_id=1, replica_groups=mesh['expert'=8,'row'=4] {'row'}, use_global_device_ids=true, to_apply=%region_11.12 | all-reduce | flops 1 | bytes 8 | tf_op jit(solution)/shard_map/psum | solution.py:121
  688.5 12.4 %psum.15 = f32[]{:T(128)} all-reduce(f32[]{:T(128)} %bitcast.31), channel_id=1, replica_groups=mesh['expert'=8,'row'=4] {'expert'}, use_global_device_ids=true, to_apply=%region_12.13 | all-reduce | flops 1 | bytes 8 | tf_op jit(solution)/shard_map/psum | solution.py:122
  (6 shorter events, 0.0 us)
Async XLA Ops:
  44.8 164.3 %collective-permute-start.1 = (bf16[1,14,128,2048]{3,2,1,0:T(8,128)(2,1)}, bf16[1,14,128,2048]{3,2,1,0:T(8,128)(2,1)}, u32[]{:S(2)}, u32[]{:S(2)}) collective-permute-start(bf16[1,14,128,2048]{3,2,1,0:T(8,128)(2,1)} %convert_element_type.90), channel_id=1, source_target_pairs={{0,1},{1,2},{2,3},{3,0},{4,5},{5,6},{6,7},{7,4},{8,9},{9,10},{10,1... | collective-permute-start | bytes 22020104 | tf_op jit(solution)/shard_map/ppermute | solution.py:95
  47.9 317.3 %collective-permute-start = (bf16[1,14,128,2048]{3,2,1,0:T(8,128)(2,1)}, bf16[1,14,128,2048]{3,2,1,0:T(8,128)(2,1)}, u32[]{:S(2)}, u32[]{:S(2)}) collective-permute-start(bf16[1,14,128,2048]{3,2,1,0:T(8,128)(2,1)} %convert_element_type.90), channel_id=1, source_target_pairs={{0,3},{1,0},{2,1},{3,2},{4,7},{5,4},{6,5},{7,6},{8,11},{9,8},{10,9... | collective-permute-start | bytes 22020104 | tf_op jit(solution)/shard_map/ppermute | solution.py:97
  209.1 313.7 %collective-permute-start.2 = (bf16[1,14,128,2048]{3,2,1,0:T(8,128)(2,1)}, bf16[1,14,128,2048]{3,2,1,0:T(8,128)(2,1)}, u32[]{:S(2)}, u32[]{:S(2)}) collective-permute-start(bf16[1,14,128,2048]{3,2,1,0:T(8,128)(2,1)} %collective-permute-done.1), channel_id=1, source_target_pairs={{0,1},{1,2},{2,3},{3,0},{4,5},{5,6},{6,7},{7,4},{8,9},{9,10},{10,1... | collective-permute-start | bytes 22020104 | tf_op jit(solution)/shard_map/ppermute | solution.py:95
  554.7 29.8 %copy-start = (s32[1,2048]{1,0:T(1,128)S(1)}, s32[1,2048]{1,0:T(1,128)}, u32[]{:S(2)}) copy-start(s32[1,2048]{1,0:T(1,128)} %param.7) | copy-start | bytes 24580
